TPU v7x, 32 devices: a whole 2x2x4 slice. The times are simulated.
32 devices in a mesh: gz: 8 (over z, y), pa: 4 (over x, core).
Axes of the slice: x: 2, y: 2, z: 4, core: 2. Of those that a mesh axis runs over, the one named last changes fastest.
Arguments:
- density: bfloat16 [64, 1024, 1024], P('gz', 'pa'), may hold values from -6 to 6
- green: float32 [128, 1024, 1024], P('gz', 'pa'), may hold values from 0.1 to 3
Outputs:
- potential: float32 [64, 1024, 1024], P('gz', 'pa')
All inputs are finite; a program needn't handle non-finite values.
Results may differ from a plain program's by a relative error of at most 0.02.
Values may be sent and summed in bfloat16 or wider, within the bound.
A program may use at most 192 MiB of HBM per device.

v0:
```python
import math

import jax
import jax.numpy as jnp
from jax import lax
from jax.sharding import PartitionSpec as P


def cas_table(rows, cols, length):
    product = rows[:, None] * cols[None, :] % length
    angle = product.astype(jnp.float32) * (2.0 * math.pi / length)
    return (jnp.cos(angle) + jnp.sin(angle)).astype(jnp.bfloat16)


def grouped_sum(tables, pieces):
    terms = jnp.einsum("gkz,gzs->gks", tables, pieces, preferred_element_type=jnp.float32).astype(
        jnp.bfloat16
    )
    terms = lax.optimization_barrier(terms)
    return jnp.sum(terms.astype(jnp.float32), axis=0)


def local(density, green):
    z_slab, x_local, y_cells = density.shape
    k_block, y_local, x_cells = green.shape
    groups = lax.axis_size("gz")
    pencils = lax.axis_size("pa")
    z_cells = z_slab * groups
    z_freqs = k_block * groups
    columns = x_local * y_cells
    f_index = jnp.arange(z_freqs, dtype=jnp.int32)
    z_index = jnp.arange(z_cells, dtype=jnp.int32)
    flat = density.reshape(z_slab, columns)
    planes = lax.all_to_all(flat, "gz", split_axis=1, concat_axis=0, tiled=True)
    share = planes.shape[1]
    tables = (
        cas_table(f_index, z_index, z_freqs).reshape(z_freqs, groups, z_slab).transpose(1, 0, 2)
    )
    slabs = planes.reshape(groups, z_slab, share)
    spectrum = grouped_sum(tables, slabs).astype(jnp.bfloat16)
    zspec = lax.all_to_all(spectrum, "gz", split_axis=0, concat_axis=1, tiled=True).reshape(
        k_block, x_local, y_cells
    )
    cas_y = cas_table(
        jnp.arange(y_cells, dtype=jnp.int32), jnp.arange(y_cells, dtype=jnp.int32), y_cells
    )
    cas_x = cas_table(
        jnp.arange(x_cells, dtype=jnp.int32), jnp.arange(x_cells, dtype=jnp.int32), x_cells
    )
    yspec = jnp.einsum("kxy,vy->vkx", zspec, cas_y, preferred_element_type=jnp.float32).astype(
        jnp.bfloat16
    )
    yspec = yspec.reshape(y_cells, k_block * x_local)
    moved = lax.all_to_all(yspec, "pa", split_axis=0, concat_axis=1, tiled=True).reshape(
        y_local, pencils, k_block, x_local
    )
    xspec = jnp.einsum(
        "vskl,usl->kvu",
        moved,
        cas_x.reshape(x_cells, pencils, x_local),
        preferred_element_type=jnp.float32,
    )
    weighted = (green * xspec).astype(jnp.bfloat16)
    inverted = jnp.einsum(
        "kvu,usl->vskl",
        weighted,
        cas_x.reshape(x_cells, pencils, x_local),
        preferred_element_type=jnp.float32,
    )
    inverted = inverted.astype(jnp.bfloat16).reshape(y_local, pencils * k_block * x_local)
    returned = lax.all_to_all(inverted, "pa", split_axis=1, concat_axis=0, tiled=True).reshape(
        y_cells, k_block, x_local
    )
    zback = jnp.einsum("vkl,yv->kly", returned, cas_y, preferred_element_type=jnp.float32).astype(
        jnp.bfloat16
    )
    scale = 1.0 / (x_cells * y_cells * z_freqs)
    flat_back = zback.reshape(k_block, columns)
    spectra = lax.all_to_all(flat_back, "gz", split_axis=1, concat_axis=0, tiled=True)
    share = spectra.shape[1]
    tables = (
        cas_table(z_index, f_index, z_freqs).reshape(z_cells, groups, k_block).transpose(1, 0, 2)
    )
    blocks = spectra.reshape(groups, k_block, share)
    total = grouped_sum(tables, blocks) * scale
    potential = (
        lax.all_to_all(total.astype(jnp.bfloat16), "gz", split_axis=0, concat_axis=1, tiled=True)
        .astype(total.dtype)
        .reshape(z_slab, x_local, y_cells)
    )
    return potential


def solution(mesh):
    return jax.shard_map(
        local,
        mesh=mesh,
        in_specs=(P("gz", "pa", None), P("gz", "pa", None)),
        out_specs=P("gz", "pa", None),
        check_vma=False,
    )
```

profile of v0, /device:TPU:0, one launch (start us, length us, event | category | flops | bytes accessed | tf_op | source)
XLA Modules:
  0.0 1125.3 jit_solution(10783536382925773258)
XLA Ops:
  0.0 7.4 all_to_all.68
  7.4 6.4 copy.19
  13.8 7.3 all-to-all-start
  21.1 93.3 %all-to-all-done = bf16[8,8,32768]{2,0,1:T(8,128)(2,1)} async-done(((bf16[8,8,32768]{2,0,1:T(8,128)(2,1)}), bf16[8,8,32768]{2,0,1:T(8,128)(2,1)}, u32[]{:S(2)}, u32[]{:S(2)}) %all-to-all-start) | async-done | bytes 4194336 | tf_op jit(solution)/shard_map/all_to_all | solution.py:34
  114.4 27.0 %convolution_convert_fusion = bf16[8,128,32768]{2,1,0:T(8,128)(2,1)} fusion(bf16[8,8,32768]{2,0,1:T(8,128)(2,1)} %all-to-all-done, s32[8,8]{1,0:T(8,128)S(1)} %multiply_add_fusion), kind=kOutput, calls=%fused_computation.1 | convolution fusion | flops 570556416 | bytes 71303424 | tf_op jit(solution)/shard_map/gkz,gzs->gks/dot_general | solution.py:16
  141.3 26.0 %reduce_sum.21 = bf16[128,32768]{1,0:T(8,128)(2,1)} reduce(bf16[8,128,32768]{2,1,0:T(8,128)(2,1)} %convolution_convert_fusion, bf16[]{:T(256)} %constant.56.clone.1), dimensions={0}, to_apply=%region_0.1 | reduce | flops 29360128 | bytes 75497472 | tf_op jit(solution)/shard_map/reduce_sum | solution.py:20
  167.3 199.8 %all_to_all.90 = bf16[8,16,32768]{2,1,0:T(8,128)(2,1)} all-to-all(bf16[8,16,32768]{2,1,0:T(8,128)(2,1)} %bitcast.88), channel_id=1, replica_groups=mesh['gz'=8,'pa'=4] {'gz'}, dimensions={0} | all-to-all | bytes 16777216 | tf_op jit(solution)/shard_map/all_to_all | solution.py:41
  367.1 11.4 %copy.20 = bf16[16,8,32768]{2,1,0:T(8,128)(2,1)} copy(bf16[16,8,32768]{2,0,1:T(8,128)(2,1)} %bitcast.87) | data formatting | bytes 16777216 | tf_op jit(solution)/shard_map/all_to_all | solution.py:41
  378.5 13.5 %reshape.90 = bf16[16,256,1024]{2,1,0:T(8,128)(2,1)} reshape(bf16[16,8,32768]{2,1,0:T(8,128)(2,1)} %copy.20) | data formatting | bytes 16777216 | tf_op jit(solution)/shard_map/reshape | solution.py:41
  392.0 30.5 %convolution_convert_fusion.2 = bf16[1024,16,256]{2,0,1:T(8,128)(2,1)} fusion(bf16[16,256,1024]{2,1,0:T(8,128)(2,1)} %reshape.90), kind=kOutput, calls=%fused_computation.10 | convolution fusion | flops 8610906112 | bytes 16777216 | tf_op jit(solution)/shard_map/kxy,vy->vkx/dot_general | solution.py:50
  422.6 11.4 %copy.21 = bf16[1024,16,256]{2,1,0:T(8,128)(2,1)} copy(bf16[1024,16,256]{2,0,1:T(8,128)(2,1)} %convolution_convert_fusion.2) | data formatting | bytes 16777216 | tf_op jit(solution)/shard_map/convert_element_type | solution.py:50
  434.0 13.4 %all_to_all.74 = bf16[4,256,4096]{2,1,0:T(8,128)(2,1)} reshape(bf16[1024,16,256]{2,1,0:T(8,128)(2,1)} %copy.21) | data formatting | bytes 16777216 | tf_op jit(solution)/shard_map/all_to_all | solution.py:54
  447.4 5.6 all-to-all-start.2
  453.0 17.6 %copy.25 = f32[16,256,1024]{1,2,0:T(8,128)} copy(f32[16,256,1024]{2,1,0:T(8,128)} %param.3) | data formatting | bytes 33554432 | tf_op args[1]
  470.7 75.5 %all-to-all-done.2 = bf16[4,256,4096]{2,1,0:T(8,128)(2,1)} async-done(((bf16[4,256,4096]{2,1,0:T(8,128)(2,1)}), bf16[4,256,4096]{2,1,0:T(8,128)(2,1)}, u32[]{:S(2)}, u32[]{:S(2)}) %all-to-all-start.2) | async-done | bytes 8388640 | tf_op jit(solution)/shard_map/all_to_all | solution.py:54
  546.2 11.9 %copy.22 = bf16[256,4,4096]{0,2,1:T(8,128)(2,1)} copy(bf16[256,4,4096]{2,0,1:T(8,128)(2,1)} %bitcast.7) | data formatting | bytes 16777216 | tf_op jit(solution)/shard_map/all_to_all | solution.py:54
  558.1 33.0 %fusion.113 = bf16[16,256,1024,1]{1,2,0,3:T(8,128)(2,1)} fusion(f32[16,256,1024]{1,2,0:T(8,128)} %copy.25, bf16[256,4,16,256]{0,3,2,1:T(8,128)(2,1)} %bitcast.90, s32[4,256]{1,0:T(4,128)S(1)} %multiply_add_fusion.1), kind=kOutput, calls=%fused_computation.7.clone.clone.clone.2 | convolution fusion | flops 8615100416 | bytes 33558528 | tf_op jit(solution)/shard_map/vskl,usl->kvu/dot_general | solution.py:57
  591.1 30.0 %fusion.4 = bf16[4,256,16,256]{3,1,2,0:T(8,128)(2,1)} fusion(s32[4,256]{1,0:T(4,128)S(1)} %multiply_add_fusion.1, bf16[16,256,1024,1]{1,2,0,3:T(8,128)(2,1)} %fusion.113), kind=kOutput, calls=%fused_computation.11 | convolution fusion | flops 8610906112 | bytes 16781312 | tf_op jit(solution)/shard_map/kvu,usl->vskl/dot_general | solution.py:64
  621.1 5.6 all-to-all-start.3
  626.8 16.9 %fusion.115 = bf16[1024,1024,1]{1,0,2:T(8,128)(2,1)S(1)} fusion(), kind=kLoop, calls=%fused_computation.36.clone.clone.1 | loop fusion | flops 16777216 | bytes 2097152 | tf_op jit(solution)/shard_map/vkl,yv->kly/dot_general | solution.py:74
  643.7 76.2 %all-to-all-done.3 = bf16[256,4,4096]{0,2,1:T(8,128)(2,1)} async-done(((bf16[256,4,4096]{0,2,1:T(8,128)(2,1)}), bf16[256,4,4096]{0,2,1:T(8,128)(2,1)}, u32[]{:S(2)}, u32[]{:S(2)}) %all-to-all-start.3) | async-done | bytes 8388640 | tf_op jit(solution)/shard_map/all_to_all | solution.py:71
  719.9 12.1 %copy.27 = bf16[4,256,4096]{1,0,2:T(4,128)(2,1)} copy(bf16[4,256,4096]{1,2,0:T(8,128)(2,1)} %bitcast.15) | data formatting | bytes 16777216 | tf_op jit(solution)/shard_map/all_to_all | solution.py:71
  732.1 14.3 %reshape.92 = bf16[1024,16,256]{0,2,1:T(8,128)(2,1)} reshape(bf16[4,256,4096]{1,0,2:T(4,128)(2,1)} %copy.27) | data formatting | bytes 16777216 | tf_op jit(solution)/shard_map/reshape | solution.py:71
  746.3 14.5 %convolution_convert_fusion.3 = bf16[16,256,1024]{2,1,0:T(8,128)(2,1)} fusion(bf16[1024,16,256]{0,2,1:T(8,128)(2,1)} %reshape.92, bf16[1024,1024,1]{1,0,2:T(8,128)(2,1)S(1)} %fusion.115), kind=kOutput, calls=%fused_computation.12 | convolution fusion | flops 8594128896 | bytes 18874368 | tf_op jit(solution)/shard_map/vkl,yv->kly/dot_general | solution.py:74
  760.9 13.7 %all_to_all.80 = bf16[16,8,32768]{2,1,0:T(8,128)(2,1)} reshape(bf16[16,256,1024]{2,1,0:T(8,128)(2,1)} %convolution_convert_fusion.3) | data formatting | bytes 16777216 | tf_op jit(solution)/shard_map/all_to_all | solution.py:79
  774.6 11.4 %copy.28 = bf16[16,8,32768]{2,0,1:T(8,128)(2,1)} copy(bf16[16,8,32768]{2,1,0:T(8,128)(2,1)} %all_to_all.80) | data formatting | bytes 16777216 | tf_op jit(solution)/shard_map/all_to_all | solution.py:79
  786.0 5.0 all-to-all-start.4
  791.0 183.0 %all-to-all-done.4 = bf16[16,8,32768]{2,0,1:T(8,128)(2,1)} async-done(((bf16[16,8,32768]{2,0,1:T(8,128)(2,1)}), bf16[16,8,32768]{2,0,1:T(8,128)(2,1)}, u32[]{:S(2)}, u32[]{:S(2)}) %all-to-all-start.4) | async-done | bytes 8388640 | tf_op jit(solution)/shard_map/all_to_all | solution.py:79
  974.0 17.0 %convolution_convert_fusion.1 = bf16[8,64,32768]{2,1,0:T(8,128)(2,1)} fusion(bf16[16,8,32768]{2,0,1:T(8,128)(2,1)} %all-to-all-done.4, s32[8,16]{1,0:T(8,128)S(1)} %multiply_add_fusion.2), kind=kOutput, calls=%fused_computation.2 | convolution fusion | flops 553779200 | bytes 41943552 | tf_op jit(solution)/shard_map/gkz,gzs->gks/dot_general | solution.py:16
  991.0 15.1 %convert_reduce_fusion = f32[64,32768]{1,0:T(8,128)} fusion(bf16[8,64,32768]{2,1,0:T(8,128)(2,1)} %convolution_convert_fusion.1), kind=kLoop, calls=%fused_computation | loop fusion | flops 31457280 | bytes 41943040 | tf_op jit(solution)/shard_map/reduce_sum | solution.py:20
  1006.1 3.8 fusion.13
  1009.9 97.0 %all_to_all.91 = bf16[8,8,32768]{2,1,0:T(8,128)(2,1)S(1)} all-to-all(bf16[8,8,32768]{2,1,0:T(8,128)(2,1)S(1)} %fusion.13), channel_id=1, replica_groups=mesh['gz'=8,'pa'=4] {'gz'}, dimensions={0} | all-to-all | bytes 8388608 | tf_op jit(solution)/shard_map/all_to_all | solution.py:87
  1106.9 0.5 convert_bitcast_fusion
  1107.5 8.1 copy.29
  1115.5 9.4 reshape.93
  (3 shorter events, 0.0 us)
Async XLA Ops:
  13.8 100.6 %all-to-all-start = ((bf16[8,8,32768]{2,0,1:T(8,128)(2,1)}), bf16[8,8,32768]{2,0,1:T(8,128)(2,1)}, u32[]{:S(2)}, u32[]{:S(2)}) async-start(bf16[8,8,32768]{2,0,1:T(8,128)(2,1)} %copy.19), calls=%async_computation | async-start | bytes 8388608 | tf_op jit(solution)/shard_map/all_to_all | solution.py:34
  447.4 98.8 %all-to-all-start.2 = ((bf16[4,256,4096]{2,1,0:T(8,128)(2,1)}), bf16[4,256,4096]{2,1,0:T(8,128)(2,1)}, u32[]{:S(2)}, u32[]{:S(2)}) async-start(bf16[4,256,4096]{2,1,0:T(8,128)(2,1)} %all_to_all.74), calls=%async_computation.2 | async-start | bytes 16777216 | tf_op jit(solution)/shard_map/all_to_all | solution.py:54
  621.1 98.8 %all-to-all-start.3 = ((bf16[256,4,4096]{0,2,1:T(8,128)(2,1)}), bf16[256,4,4096]{0,2,1:T(8,128)(2,1)}, u32[]{:S(2)}, u32[]{:S(2)}) async-start(bf16[256,4,4096]{0,2,1:T(8,128)(2,1)} %bitcast.89), calls=%async_computation.3 | async-start | bytes 16777216 | tf_op jit(solution)/shard_map/all_to_all | solution.py:71
  786.0 188.0 %all-to-all-start.4 = ((bf16[16,8,32768]{2,0,1:T(8,128)(2,1)}), bf16[16,8,32768]{2,0,1:T(8,128)(2,1)}, u32[]{:S(2)}, u32[]{:S(2)}) async-start(bf16[16,8,32768]{2,0,1:T(8,128)(2,1)} %copy.28), calls=%async_computation.4 | async-start | bytes 16777216 | tf_op jit(solution)/shard_map/all_to_all | solution.py:79
where the time goes:
time: 1140 us; the launch traced here: 1130 us
  waiting for transfers between devices  428 us (38%)
  blocking collectives  297 us (26%)
  local copies, waits for them, and re-layouts  162 us (14%)
  matrix products  152 us (13%)
  other arithmetic  62.4 us (5%)
  starting transfers between devices  23.5 us (2%)
    all_to_all x1, blocking collectives, local(): lax.all_to_all(spectrum, 'gz', split_axis=0, concat_axis=1, tiled=True)  200 us
    all_to_all x1, waiting for transfers between devices, local(): lax.all_to_all(flat_back, 'gz', split_axis=1, concat_axis=0, tiled=True)  183 us
    all_to_all x1, blocking collectives, local(): lax.all_to_all(total.astype(jnp.bfloat16), 'gz', split_axis=0, concat_axi...  97 us
    all_to_all x1, waiting for transfers between devices, local(): planes = lax.all_to_all(flat, 'gz', split_axis=1, concat_axis=0, tiled=True)  93.3 us
    all_to_all x1, waiting for transfers between devices, local(): lax.all_to_all(inverted, 'pa', split_axis=1, concat_axis=0, tiled=True)  76.2 us
    all_to_all x1, waiting for transfers between devices, local(): lax.all_to_all(yspec, 'pa', split_axis=0, concat_axis=1, tiled=True)  75.5 us
    dot_general x2, matrix products, grouped_sum(): jnp.einsum('gkz,gzs->gks', tables, pieces, preferred_element_type=jnp.flo...  44 us
    reduce_sum x2, other arithmetic, grouped_sum(): return jnp.sum(terms.astype(jnp.float32), axis=0)  41.1 us
  transfers between devices with their start and end apart: 4, of which 4 were waited for; matrix products, arithmetic and copies ran while one was open for 3% of the time, Pallas kernels for 0%

commit v1 on v0

v1 whole, which is shorter than its diff:
```python
import math

import jax
import jax.numpy as jnp
from jax import lax
from jax.experimental import pallas as pl
from jax.experimental.pallas import tpu as pltpu
from jax.sharding import PartitionSpec as P

BF = jnp.bfloat16
F32 = jnp.float32


def cas_table(rows, cols, length):
    product = rows[:, None] * cols[None, :] % length
    angle = product.astype(F32) * (2.0 * math.pi / length)
    return (jnp.cos(angle) + jnp.sin(angle)).astype(BF)


def square_table(n):
    index = jnp.arange(n, dtype=jnp.int32)
    return cas_table(index, index, n)


def cost(flops, *arrays):
    size = sum(math.prod(a.shape) * a.dtype.itemsize for a in arrays)
    return pl.CostEstimate(flops=flops, bytes_accessed=size, transcendentals=0)


def dot(a, b):
    return jnp.dot(a, b, preferred_element_type=F32)


def dot_t(a, b):
    return lax.dot_general(a, b, (((1,), (1,)), ((), ())), preferred_element_type=F32)


def green_split(green, groups):
    k, v, u = green.shape
    share = v // groups

    def body(g_ref, o_ref):
        for j in range(groups):
            o_ref[j, 0] = g_ref[0, j * share : (j + 1) * share, :].astype(BF)

    out = jax.ShapeDtypeStruct((groups, k, share, u), BF)
    return pl.pallas_call(
        body,
        grid=(k,),
        in_specs=[pl.BlockSpec((1, v, u), lambda i: (i, 0, 0))],
        out_specs=pl.BlockSpec((groups, 1, share, u), lambda i: (0, i, 0, 0)),
        out_shape=out,
        cost_estimate=cost(0, green, out),
        name="green_split",
    )(green)


def y_forward(density, table, pencils):
    z, x, y = density.shape
    block = y // pencils

    def body(d_ref, t_ref, o_ref):
        for p in range(pencils):
            rows = t_ref[p * block : (p + 1) * block, :]
            o_ref[p, 0] = dot_t(rows, d_ref[0]).astype(BF)

    out = jax.ShapeDtypeStruct((pencils, z, block, x), BF)
    return pl.pallas_call(
        body,
        grid=(z,),
        in_specs=[
            pl.BlockSpec((1, x, y), lambda i: (i, 0, 0)),
            pl.BlockSpec((y, y), lambda i: (0, 0)),
        ],
        out_specs=pl.BlockSpec((pencils, 1, block, x), lambda i: (0, i, 0, 0)),
        out_shape=out,
        cost_estimate=cost(2 * z * x * y * y, density, table, out),
        name="y_forward",
    )(density, table)


def x_forward(moved, table, groups):
    pencils, z, v, x = moved.shape
    u = pencils * x
    share = v // groups

    def body(m_ref, t_ref, o_ref):
        total = dot(m_ref[0, 0], t_ref[0:x, :])
        for p in range(1, pencils):
            total += dot(m_ref[p, 0], t_ref[p * x : (p + 1) * x, :])
        total = total.astype(BF)
        for j in range(groups):
            o_ref[j, 0] = total[j * share : (j + 1) * share, :]

    out = jax.ShapeDtypeStruct((groups, z, share, u), BF)
    return pl.pallas_call(
        body,
        grid=(z,),
        in_specs=[
            pl.BlockSpec((pencils, 1, v, x), lambda i: (0, i, 0, 0)),
            pl.BlockSpec((u, u), lambda i: (0, 0)),
        ],
        out_specs=pl.BlockSpec((groups, 1, share, u), lambda i: (0, i, 0, 0)),
        out_shape=out,
        cost_estimate=cost(2 * z * v * u * u, moved, table, out),
        name="x_forward",
    )(moved, table)


def z_weight(planes, green, table):
    z, v, u = planes.shape
    k = green.shape[0]
    if v % 8:
        spec = jnp.einsum("kz,zvu->kvu", table, planes, preferred_element_type=F32)
        weighted = (green.astype(F32) * spec).astype(BF)
        return jnp.einsum("kz,kvu->zvu", table, weighted, preferred_element_type=F32).astype(BF)
    lanes = min(u, 512)
    rows = 16 if v % 16 == 0 else 8
    eye = jnp.eye(8, dtype=BF)
    wide = jnp.einsum("kz,ab->kazb", table, eye).reshape(k * 8, z * 8)
    tall = wide.T

    def body(s_ref, g_ref, w_ref, t_ref, o_ref):
        for i in range(0, rows, 8):
            flat = s_ref[:, i : i + 8, :].astype(F32).reshape(z * 8, lanes).astype(BF)
            spec = dot(w_ref[...], flat)
            weight = g_ref[:, i : i + 8, :].astype(F32).reshape(k * 8, lanes)
            back = dot(t_ref[...], (spec * weight).astype(BF))
            o_ref[:, i : i + 8, :] = back.reshape(z, 8, lanes).astype(BF)

    out = jax.ShapeDtypeStruct((z, v, u), BF)
    at = lambda i, j: (0, i, j)
    whole = lambda i, j: (0, 0)
    return pl.pallas_call(
        body,
        grid=(v // rows, u // lanes),
        in_specs=[
            pl.BlockSpec((z, rows, lanes), at),
            pl.BlockSpec((k, rows, lanes), at),
            pl.BlockSpec((k * 8, z * 8), whole),
            pl.BlockSpec((z * 8, k * 8), whole),
        ],
        out_specs=pl.BlockSpec((z, rows, lanes), at),
        out_shape=out,
        compiler_params=pltpu.CompilerParams(vmem_limit_bytes=60 * 2**20),
        cost_estimate=cost(32 * z * k * v * u, planes, green, out),
        name="z_weight",
    )(planes, green, wide, tall)


def x_inverse(back, table, pencils):
    groups, z, share, u = back.shape
    v = groups * share
    x = u // pencils

    def body(b_ref, t_ref, o_ref):
        rows = jnp.concatenate([b_ref[j, 0] for j in range(groups)], axis=0)
        for p in range(pencils):
            o_ref[p, 0] = dot_t(t_ref[p * x : (p + 1) * x, :], rows).astype(BF)

    out = jax.ShapeDtypeStruct((pencils, z, x, v), BF)
    return pl.pallas_call(
        body,
        grid=(z,),
        in_specs=[
            pl.BlockSpec((groups, 1, share, u), lambda i: (0, i, 0, 0)),
            pl.BlockSpec((u, u), lambda i: (0, 0)),
        ],
        out_specs=pl.BlockSpec((pencils, 1, x, v), lambda i: (0, i, 0, 0)),
        out_shape=out,
        cost_estimate=cost(2 * z * v * u * u, back, table, out),
        name="x_inverse",
    )(back, table)


def y_inverse(returned, table, scale):
    pencils, z, x, v = returned.shape
    y = pencils * v

    def body(r_ref, t_ref, o_ref):
        total = dot(r_ref[0, 0], t_ref[0:v, :])
        for p in range(1, pencils):
            total += dot(r_ref[p, 0], t_ref[p * v : (p + 1) * v, :])
        o_ref[0] = total * scale

    out = jax.ShapeDtypeStruct((z, x, y), F32)
    return pl.pallas_call(
        body,
        grid=(z,),
        in_specs=[
            pl.BlockSpec((pencils, 1, x, v), lambda i: (0, i, 0, 0)),
            pl.BlockSpec((y, y), lambda i: (0, 0)),
        ],
        out_specs=pl.BlockSpec((1, x, y), lambda i: (i, 0, 0)),
        out_shape=out,
        cost_estimate=cost(2 * z * x * y * y, returned, table, out),
        name="y_inverse",
    )(returned, table)


def exchange(a, axis):
    return lax.all_to_all(a, axis, split_axis=0, concat_axis=0, tiled=True)


def local(density, green):
    z_slab, x_local, y_cells = density.shape
    k_block, y_local, x_cells = green.shape
    groups = lax.axis_size("gz")
    pencils = lax.axis_size("pa")
    z_cells = z_slab * groups
    z_freqs = k_block * groups
    share = y_local // groups
    weights = exchange(green_split(green, groups), "gz").reshape(z_freqs, share, x_cells)
    cas_y = square_table(y_cells)
    cas_x = cas_y if x_cells == y_cells else square_table(x_cells)
    cas_m = cas_table(
        jnp.arange(z_freqs, dtype=jnp.int32), jnp.arange(z_cells, dtype=jnp.int32), z_freqs
    )
    moved = exchange(y_forward(density, cas_y, pencils), "pa")
    planes = exchange(x_forward(moved, cas_x, groups), "gz").reshape(z_cells, share, x_cells)
    back = z_weight(planes, weights, cas_m).reshape(groups, z_slab, share, x_cells)
    back = exchange(back, "gz")
    returned = exchange(x_inverse(back, cas_x, pencils), "pa")
    return y_inverse(returned, cas_y, 1.0 / (x_cells * y_cells * z_freqs))


def solution(mesh):
    return jax.shard_map(
        local,
        mesh=mesh,
        in_specs=(P("gz", "pa", None), P("gz", "pa", None)),
        out_specs=P("gz", "pa", None),
        check_vma=False,
    )
```

time: 1140 us -> 566 us (0.50); the launches traced: 1130 us -> 564 us
  waiting for transfers between devices: 428 us -> 228 us
  matrix products: 152 us -> 0 us
  local copies, waits for them, and re-layouts: 162 us -> 25.9 us
  blocking collectives: 297 us -> 206 us
  Pallas kernels: 0 us -> 68.7 us
  other arithmetic: 62.4 us -> 23.9 us
  starting transfers between devices: 23.5 us -> 11.6 us
    all_to_all x4 -> x2, waiting for transfers between devices: 428 us -> 228 us  [exchange(): return lax.all_to_all(a, axis, split_axis=0, concat_axis=0, tiled=True)]
    dot_general x6 -> x0, matrix products: 152 us -> none  [the longest x2 44 us: grouped_sum(): jnp.einsum('gkz,gzs->gks', tables, pieces, preferred_element_type=jnp.flo...]
    all_to_all x2 -> x3, blocking collectives: 297 us -> 206 us  [exchange(): return lax.all_to_all(a, axis, split_axis=0, concat_axis=0, tiled=True)]
    all_to_all x8 -> x0, local copies, waits for them, and re-layouts: 87.7 us -> none  [the longest x2 25.4 us: local(): lax.all_to_all(yspec, 'pa', split_axis=0, concat_axis=1, tiled=True)]
    pallas_call x0 -> x6, Pallas kernels: none -> 68.7 us  [the longest x1 14.7 us: green_split(): pl.pallas_call(body, grid=(k,), in_specs=[pl.BlockSpec((1, v, u), lambda...]
    reduce_sum x2 -> x0, other arithmetic: 41.1 us -> none  [grouped_sum(): return jnp.sum(terms.astype(jnp.float32), axis=0)]
    convert_element_type x3 -> x0, local copies, waits for them, and re-layouts: 28.8 us -> none  [the longest x2 17.4 us: local(): potential = lax.all_to_all(total.astype(jnp.bfloat16), 'gz', split_axis=0...]
    unnamed x1 -> x2, local copies, waits for them, and re-layouts: 17.6 us -> 0.01 us
  transfers between devices with their start and end apart: 4 -> 2, of which waited for: 4 -> 2; matrix products, arithmetic and copies ran while one was open for 3% -> 6% of each run, Pallas kernels for 0% -> 3%
where the time goes in v1:
time: 566 us; the launch traced here: 564 us
  waiting for transfers between devices  228 us (40%)
  blocking collectives  206 us (36%)
  Pallas kernels  68.7 us (12%)
  local copies, waits for them, and re-layouts  25.9 us (5%)
  other arithmetic  23.9 us (4%)
  starting transfers between devices  11.6 us (2%)
    all_to_all x2, waiting for transfers between devices, exchange(): return lax.all_to_all(a, axis, split_axis=0, concat_axis=0, tiled=True)  228 us
    all_to_all x3, blocking collectives, exchange(): return lax.all_to_all(a, axis, split_axis=0, concat_axis=0, tiled=True)  206 us
    reshape x2, local copies, waits for them, and re-layouts, z_weight(): wide = jnp.einsum('kz,ab->kazb', table, eye).reshape(k * 8, z * 8)  25.9 us
    convert_element_type x2, other arithmetic, cas_table(): return (jnp.cos(angle) + jnp.sin(angle)).astype(BF)  17.9 us
    pallas_call x1, Pallas kernels, green_split(): pl.pallas_call(body, grid=(k,), in_specs=[pl.BlockSpec((1, v, u), lambda...  14.7 us
    pallas_call x1, Pallas kernels, z_weight(): pl.pallas_call(body, grid=(v // rows, u // lanes), in_specs=[pl.BlockSpec...  13 us
    all_to_all x2, starting transfers between devices, exchange(): return lax.all_to_all(a, axis, split_axis=0, concat_axis=0, tiled=True)  11.6 us
  transfers between devices with their start and end apart: 2, of which 2 were waited for; matrix products, arithmetic and copies ran while one was open for 6% of the time, Pallas kernels for 3%

profile of v1, /device:TPU:0, one launch (start us, length us, event | category | flops | bytes accessed | tf_op | source)
XLA Modules:
  0.0 564.0 jit_solution(6498654833693442475)
XLA Ops:
  0.0 17.6 %add_convert_fusion.t_ref = bf16[1024,1024]{1,0:T(8,128)(2,1)} fusion(), kind=kLoop, calls=%fused_computation.7 | loop fusion | flops 16777216 | bytes 2097152 | tf_op jit(solution)/shard_map/convert_element_type | solution.py:17
  17.6 10.2 %y_forward.1 = bf16[4,8,256,256]{3,2,1,0:T(8,128)(2,1)} custom-call(bf16[8,256,1024]{2,1,0:T(8,128)(2,1)} %d_ref.1, bf16[1024,1024]{1,0:T(8,128)(2,1)} %add_convert_fusion.t_ref), custom_call_target="tpu_custom_call" | custom-call | flops 4294967296 | bytes 10485760 | tf_op jit(solution)/shard_map/y_forward/pallas_call | solution.py:68
  27.8 54.5 %all_to_all.25.m_ref = bf16[4,8,256,256]{3,2,1,0:T(8,128)(2,1)} all-to-all(bf16[4,8,256,256]{3,2,1,0:T(8,128)(2,1)} %y_forward.1), channel_id=1, replica_groups=mesh['gz'=8,'pa'=4] {'pa'}, dimensions={0} | all-to-all | bytes 8388608 | tf_op jit(solution)/shard_map/all_to_all | solution.py:202
  82.3 10.0 %x_forward.1 = bf16[8,8,32,1024]{3,2,1,0:T(8,128)(2,1)} custom-call(bf16[4,8,256,256]{3,2,1,0:T(8,128)(2,1)} %all_to_all.25.m_ref, bf16[1024,1024]{1,0:T(8,128)(2,1)} %add_convert_fusion.t_ref), custom_call_target="tpu_custom_call" | custom-call | flops 4294967296 | bytes 10485760 | tf_op jit(solution)/shard_map/x_forward/pallas_call | solution.py:96
  92.4 6.6 %all-to-all-start.1 = ((bf16[8,8,32,1024]{3,2,1,0:T(8,128)(2,1)}), bf16[8,8,32,1024]{3,2,1,0:T(8,128)(2,1)}, u32[]{:S(2)}, u32[]{:S(2)}) async-start(bf16[8,8,32,1024]{3,2,1,0:T(8,128)(2,1)} %x_forward.1), calls=%async_computation.1 | async-start | bytes 8388608 | tf_op jit(solution)/shard_map/all_to_all | solution.py:202
  99.0 14.7 %green_split.1 = bf16[8,16,32,1024]{3,2,1,0:T(8,128)(2,1)} custom-call(f32[16,256,1024]{2,1,0:T(8,128)} %g_ref.1), custom_call_target="tpu_custom_call" | custom-call | bytes 25165824 | tf_op jit(solution)/shard_map/green_split/pallas_call | solution.py:47
  113.7 78.2 %all-to-all-done.1 = bf16[8,8,32,1024]{3,2,1,0:T(8,128)(2,1)} async-done(((bf16[8,8,32,1024]{3,2,1,0:T(8,128)(2,1)}), bf16[8,8,32,1024]{3,2,1,0:T(8,128)(2,1)}, u32[]{:S(2)}, u32[]{:S(2)}) %all-to-all-start.1) | async-done | bytes 4194336 | tf_op jit(solution)/shard_map/all_to_all | solution.py:202
  191.9 4.9 all-to-all-start.2
  196.9 0.3 add_convert_fusion.1
  197.1 6.0 %multiply_bitcast_fusion = bf16[128,8,64,8]{3,2,1,0:T(8,128)(2,1)} fusion(bf16[128,64]{1,0:T(8,128)(2,1)S(1)} %add_convert_fusion.1, bf16[8,8]{1,0:T(8,128)(2,1)S(1)} %fusion.12), kind=kLoop, calls=%fused_computation | loop fusion | flops 524288 | bytes 1065088 | tf_op jit(solution)/shard_map/kz,ab->kazb/transpose | solution.py:120
  203.1 24.5 %reshape.14.w_ref = bf16[1024,512]{1,0:T(8,128)(2,1)S(1)} reshape(bf16[128,8,64,8]{3,2,1,0:T(8,128)(2,1)} %multiply_bitcast_fusion) | data formatting | bytes 2097152 | tf_op jit(solution)/shard_map/reshape | solution.py:120
  227.7 0.0 copy-start
  227.7 1.3 copy.4
  229.0 149.9 %all-to-all-done.2 = bf16[8,16,32,1024]{3,2,1,0:T(8,128)(2,1)} async-done(((bf16[8,16,32,1024]{3,2,1,0:T(8,128)(2,1)}), bf16[8,16,32,1024]{3,2,1,0:T(8,128)(2,1)}, u32[]{:S(2)}, u32[]{:S(2)}) %all-to-all-start.2) | async-done | bytes 8388640 | tf_op jit(solution)/shard_map/all_to_all | solution.py:202
  378.9 0.0 copy-done
  378.9 13.0 %z_weight.1 = bf16[64,32,1024]{2,1,0:T(8,128)(2,1)} custom-call(bf16[64,32,1024]{2,1,0:T(8,128)(2,1)} %bitcast.s_ref, bf16[128,32,1024]{2,1,0:T(8,128)(2,1)} %bitcast.1.g_ref, bf16[1024,512]{1,0:T(8,128)(2,1)} %copy-done, bf16[512,1024]{1,0:T(8,128)(2,1)} %bitcast.9), custom_call_target="tpu_custom_call" | custom-call | flops 8589934592 | bytes 16777216 | tf_op jit(solution)/shard_map/z_weight/pallas_call | solution.py:134
  391.9 97.5 %all_to_all.26.b_ref = bf16[8,8,32,1024]{3,2,1,0:T(8,128)(2,1)} all-to-all(bf16[8,8,32,1024]{3,2,1,0:T(8,128)(2,1)} %bitcast.8), channel_id=1, replica_groups=mesh['gz'=8,'pa'=4] {'gz'}, dimensions={0} | all-to-all | bytes 8388608 | tf_op jit(solution)/shard_map/all_to_all | solution.py:202
  489.3 10.2 %x_inverse.1 = bf16[4,8,256,256]{3,2,1,0:T(8,128)(2,1)} custom-call(bf16[8,8,32,1024]{3,2,1,0:T(8,128)(2,1)} %all_to_all.26.b_ref, bf16[1024,1024]{1,0:T(8,128)(2,1)} %add_convert_fusion.t_ref), custom_call_target="tpu_custom_call" | custom-call | flops 4294967296 | bytes 10485760 | tf_op jit(solution)/shard_map/x_inverse/pallas_call | solution.py:162
  499.5 53.8 %all_to_all.27.r_ref = bf16[4,8,256,256]{3,2,1,0:T(8,128)(2,1)} all-to-all(bf16[4,8,256,256]{3,2,1,0:T(8,128)(2,1)} %x_inverse.1), channel_id=1, replica_groups=mesh['gz'=8,'pa'=4] {'pa'}, dimensions={0} | all-to-all | bytes 8388608 | tf_op jit(solution)/shard_map/all_to_all | solution.py:202
  553.3 10.7 %y_inverse.1 = f32[8,256,1024]{2,1,0:T(8,128)} custom-call(bf16[4,8,256,256]{3,2,1,0:T(8,128)(2,1)} %all_to_all.27.r_ref, bf16[1024,1024]{1,0:T(8,128)(2,1)} %add_convert_fusion.t_ref), custom_call_target="tpu_custom_call" | custom-call | flops 4294967296 | bytes 14680064 | tf_op jit(solution)/shard_map/y_inverse/pallas_call | solution.py:187
  (1 shorter events, 0.0 us)
Async XLA Ops:
  92.4 99.5 %all-to-all-start.1 = ((bf16[8,8,32,1024]{3,2,1,0:T(8,128)(2,1)}), bf16[8,8,32,1024]{3,2,1,0:T(8,128)(2,1)}, u32[]{:S(2)}, u32[]{:S(2)}) async-start(bf16[8,8,32,1024]{3,2,1,0:T(8,128)(2,1)} %x_forward.1), calls=%async_computation.1 | async-start | bytes 8388608 | tf_op jit(solution)/shard_map/all_to_all | solution.py:202
  191.9 187.0 %all-to-all-start.2 = ((bf16[8,16,32,1024]{3,2,1,0:T(8,128)(2,1)}), bf16[8,16,32,1024]{3,2,1,0:T(8,128)(2,1)}, u32[]{:S(2)}, u32[]{:S(2)}) async-start(bf16[8,16,32,1024]{3,2,1,0:T(8,128)(2,1)} %green_split.1), calls=%async_computation.2 | async-start | bytes 16777216 | tf_op jit(solution)/shard_map/all_to_all | solution.py:202
  227.7 151.2 %copy-start = (bf16[1024,512]{1,0:T(8,128)(2,1)}, bf16[1024,512]{1,0:T(8,128)(2,1)S(1)}, u32[]{:S(2)}) copy-start(bf16[1024,512]{1,0:T(8,128)(2,1)S(1)} %reshape.14.w_ref) | copy-start | bytes 3145732

commit v2 on v1

v2 whole, which is shorter than its diff:
```python
import math

import jax
import jax.numpy as jnp
from jax import lax
from jax.experimental import pallas as pl
from jax.experimental.pallas import tpu as pltpu
from jax.sharding import PartitionSpec as P


BF = jnp.bfloat16
F32 = jnp.float32
CHUNKS = 2


def cas_table(rows, cols, length):
    product = rows[:, None] * cols[None, :] % length
    angle = product.astype(F32) * (2.0 * math.pi / length)
    return (jnp.cos(angle) + jnp.sin(angle)).astype(BF)


def square_table(n):
    index = jnp.arange(n, dtype=jnp.int32)
    return cas_table(index, index, n)


def cost(flops, *arrays):
    size = sum(math.prod(a.shape) * a.dtype.itemsize for a in arrays)
    return pl.CostEstimate(flops=flops, bytes_accessed=size, transcendentals=0)


def dot(a, b):
    return jnp.dot(a, b, preferred_element_type=F32)


def dot_t(a, b):
    return lax.dot_general(a, b, (((1,), (1,)), ((), ())), preferred_element_type=F32)


def on_rank(body, grid, in_specs, out_specs, out_shape, cost_estimate, **more):
    spec = pltpu.PrefetchScalarGridSpec(
        num_scalar_prefetch=1, grid=grid, in_specs=in_specs, out_specs=out_specs
    )
    return pl.pallas_call(
        lambda r, *refs: body(*refs),
        grid_spec=spec,
        out_shape=out_shape,
        cost_estimate=cost_estimate,
        **more,
    )


def green_piece(green, rank, step, groups):
    k, v, u = green.shape
    share = v // groups
    cut = math.gcd(k, 4)
    pieces = green.reshape(k, groups, share, u)

    def body(g_ref, o_ref):
        o_ref[...] = g_ref[:, 0].astype(BF)

    out = jax.ShapeDtypeStruct((k, share, u), BF)
    return on_rank(
        body,
        (k // cut,),
        [pl.BlockSpec((cut, 1, share, u), lambda i, r: (i, lax.rem(r[0] + step, groups), 0, 0))],
        pl.BlockSpec((cut, share, u), lambda i, r: (i, 0, 0)),
        out,
        cost(0, out, out, out),
    )(rank, pieces)


def shift(a, axis, step):
    n = lax.axis_size(axis)
    return lax.ppermute(a, axis, [(i, (i + step) % n) for i in range(n)])


def y_forward(density, table, pencils):
    z, x, y = density.shape
    block = y // pencils

    def body(d_ref, t_ref, o_ref):
        for p in range(pencils):
            rows = t_ref[p * block : (p + 1) * block, :]
            o_ref[p, 0] = dot_t(rows, d_ref[0]).astype(BF)

    out = jax.ShapeDtypeStruct((pencils, z, block, x), BF)
    return pl.pallas_call(
        body,
        grid=(z,),
        in_specs=[
            pl.BlockSpec((1, x, y), lambda i: (i, 0, 0)),
            pl.BlockSpec((y, y), lambda i: (0, 0)),
        ],
        out_specs=pl.BlockSpec((pencils, 1, block, x), lambda i: (0, i, 0, 0)),
        out_shape=out,
        cost_estimate=cost(2 * z * x * y * y, density, table, out),
        name="y_forward",
    )(density, table)


def x_forward(moved, table, groups):
    pencils, z, v, x = moved.shape
    u = pencils * x
    share = v // groups

    def body(m_ref, t_ref, o_ref):
        total = dot(m_ref[0, 0], t_ref[0:x, :])
        for p in range(1, pencils):
            total += dot(m_ref[p, 0], t_ref[p * x : (p + 1) * x, :])
        total = total.astype(BF)
        for j in range(groups):
            o_ref[j, 0] = total[j * share : (j + 1) * share, :]

    out = jax.ShapeDtypeStruct((groups, z, share, u), BF)
    return pl.pallas_call(
        body,
        grid=(z,),
        in_specs=[
            pl.BlockSpec((pencils, 1, v, x), lambda i: (0, i, 0, 0)),
            pl.BlockSpec((u, u), lambda i: (0, 0)),
        ],
        out_specs=pl.BlockSpec((groups, 1, share, u), lambda i: (0, i, 0, 0)),
        out_shape=out,
        cost_estimate=cost(2 * z * v * u * u, moved, table, out),
        name="x_forward",
    )(moved, table)


def z_weight(planes, greens, table, chunks):
    z, v, u = planes.shape
    groups = len(greens)
    part = greens[0].shape[0]
    k = part * groups
    depth = z // groups // chunks
    if v % 8:
        green = jnp.concatenate(greens, axis=0)
        spec = jnp.einsum("kz,zvu->kvu", table, planes, preferred_element_type=F32)
        weighted = (green.astype(F32) * spec).astype(BF)
        back = jnp.einsum("kz,kvu->zvu", table, weighted, preferred_element_type=F32).astype(BF)
        back = back.reshape(groups, chunks, depth, v, u)
        return [back[:, c] for c in range(chunks)]
    lanes = min(u, 512)
    rows = 16 if v % 16 == 0 else 8
    row = jnp.arange(8, dtype=jnp.int32)

    def widen(t):
        same = (jnp.arange(8 * t.shape[0]) % 8)[:, None] == (jnp.arange(8 * t.shape[1]) % 8)[None]
        return jnp.where(same, jnp.repeat(jnp.repeat(t, 8, axis=0), 8, axis=1), 0).astype(BF)

    wide = widen(table)
    tall = widen(table.T)

    def body(s_ref, *refs):
        g_refs, (w_ref, t_ref), o_refs = refs[:groups], refs[groups : groups + 2], refs[groups + 2 :]
        for i in range(0, rows, 8):
            flat = s_ref[:, i : i + 8, :].astype(F32).reshape(z * 8, lanes).astype(BF)
            spec = dot(w_ref[...], flat)
            weight = jnp.concatenate(
                [g[:, i : i + 8, :].astype(F32).reshape(part * 8, lanes) for g in g_refs], axis=0
            )
            back = dot(t_ref[...], (spec * weight).astype(BF))
            back = back.reshape(groups, chunks, depth, 8, lanes).astype(BF)
            for c in range(chunks):
                o_refs[c][:, :, i : i + 8, :] = back[:, c]

    out = jax.ShapeDtypeStruct((groups, depth, v, u), BF)
    at = lambda i, j: (0, i, j)
    whole = lambda i, j: (0, 0)
    return pl.pallas_call(
        body,
        grid=(v // rows, u // lanes),
        in_specs=[
            pl.BlockSpec((z, rows, lanes), at),
            *[pl.BlockSpec((part, rows, lanes), at)] * groups,
            pl.BlockSpec((k * 8, z * 8), whole),
            pl.BlockSpec((z * 8, k * 8), whole),
        ],
        out_specs=[pl.BlockSpec((groups, depth, rows, lanes), lambda i, j: (0, 0, i, j))] * chunks,
        out_shape=[out] * chunks,
        compiler_params=pltpu.CompilerParams(vmem_limit_bytes=60 * 2**20),
        cost_estimate=cost(32 * z * k * v * u, planes, *greens, planes),
        name="z_weight",
    )(planes, *greens, wide, tall)


def x_inverse(back, table, rank, step, pencils):
    groups, z, share, u = back.shape
    v = groups * share
    x = u // pencils

    def body(b_ref, t_ref, o_ref):
        rows = jnp.concatenate([b_ref[j, 0] for j in range(groups)], axis=0)
        o_ref[0] = dot_t(t_ref[...], rows).astype(BF)

    out = jax.ShapeDtypeStruct((z, x, v), BF)
    return on_rank(
        body,
        (z,),
        [
            pl.BlockSpec((groups, 1, share, u), lambda i, r: (0, i, 0, 0)),
            pl.BlockSpec((x, u), lambda i, r: (lax.rem(r[0] + step, pencils), 0)),
        ],
        pl.BlockSpec((1, x, v), lambda i, r: (i, 0, 0)),
        out,
        cost(2 * z * v * u * x, back, out),
    )(rank, back, table)


def y_inverse(returned, table, rank, scale, total, z_all, first):
    pencils = len(returned)
    z, x, v = returned[0].shape
    y = pencils * v

    def body(*refs):
        r_refs, t_refs, o_ref = refs[:pencils], refs[pencils : 2 * pencils], refs[-1]
        acc = dot(r_refs[0][0], t_refs[0][...])
        for p in range(1, pencils):
            acc += dot(r_refs[p][0], t_refs[p][...])
        o_ref[0] = acc * scale

    def rows_of(s):
        return lambda i, r: (lax.rem(r[0] + pencils - s, pencils), 0)

    specs = [pl.BlockSpec((1, x, v), lambda i, r: (i, 0, 0))] * pencils
    specs += [pl.BlockSpec((v, y), rows_of(s)) for s in range(pencils)]
    operands = [*returned, *[table] * pencils]
    aliases = {}
    if total is not None:
        aliases = {1 + len(operands): 0}
        specs.append(pl.BlockSpec(memory_space=pl.ANY))
        operands.append(total)
    return on_rank(
        body,
        (z,),
        specs,
        pl.BlockSpec((1, x, y), lambda i, r: (i + first, 0, 0)),
        jax.ShapeDtypeStruct((z_all, x, y), F32),
        cost(2 * z * x * y * y, *returned, *returned, *returned),
        input_output_aliases=aliases,
    )(rank, *operands)


def exchange(a, axis):
    return lax.all_to_all(a, axis, split_axis=0, concat_axis=0, tiled=True)


def local(density, green):
    z_slab, _, y_cells = density.shape
    k_block, y_local, x_cells = green.shape
    groups = lax.axis_size("gz")
    pencils = lax.axis_size("pa")
    z_cells = z_slab * groups
    z_freqs = k_block * groups
    share = y_local // groups
    g_rank = lax.axis_index("gz").astype(jnp.int32)
    p_rank = lax.axis_index("pa").astype(jnp.int32)
    g_me, p_me = g_rank.reshape(1), p_rank.reshape(1)
    greens = []
    for s in [*range(1, groups), 0]:
        piece = green_piece(green, g_me, s, groups)
        if s:
            piece = shift(piece, "gz", s)
        greens.append(piece)
    order = jnp.array([*range(1, groups), 0], dtype=jnp.int32)
    sources = (g_rank - order) % groups
    f_index = (sources[:, None] * k_block + jnp.arange(k_block, dtype=jnp.int32)).reshape(-1)
    cas_y = square_table(y_cells)
    cas_x = cas_y if x_cells == y_cells else square_table(x_cells)
    cas_m = cas_table(f_index, jnp.arange(z_cells, dtype=jnp.int32), z_freqs)
    moved = y_forward(density, cas_y, pencils)
    moved = exchange(moved, "pa")
    planes = x_forward(moved, cas_x, groups)
    planes = exchange(planes, "gz").reshape(z_cells, share, x_cells)
    chunks = math.gcd(z_slab, CHUNKS)
    scale = 1.0 / (x_cells * y_cells * z_freqs)
    potential = None
    for c, back in enumerate(z_weight(planes, greens, cas_m, chunks)):
        back = exchange(back, "gz")
        returned = [x_inverse(back, cas_x, p_me, s, pencils) for s in range(pencils)]
        returned = [shift(a, "pa", s) if s else a for s, a in enumerate(returned)]
        first = c * (z_slab // chunks)
        potential = y_inverse(returned, cas_y, p_me, scale, potential, z_slab, first)
    return potential


def solution(mesh):
    return jax.shard_map(
        local,
        mesh=mesh,
        in_specs=(P("gz", "pa", None), P("gz", "pa", None)),
        out_specs=P("gz", "pa", None),
        check_vma=False,
    )
```

time: 566 us -> 531 us (0.938)
  waiting for transfers between devices: 228 us -> 175 us
  Pallas kernels: 68.7 us -> 109 us
  blocking collectives: 206 us -> 173 us
  starting transfers between devices: 11.6 us -> 44.4 us
  local copies, waits for them, and re-layouts: 25.9 us -> 6.34 us
    all_to_all x2, waiting for transfers between devices: 228 us -> 32.8 us  [exchange(): return lax.all_to_all(a, axis, split_axis=0, concat_axis=0, tiled=True)]
    ppermute x0 -> x13, waiting for transfers between devices: none -> 142 us  [shift(): return lax.ppermute(a, axis, [(i, (i + step) % n) for i in range(n)])]
    pallas_call x3 -> x18, Pallas kernels: 35.5 us -> 76 us  [the longest x8 34.2 us: x_inverse(): on_rank(body, (z,), [pl.BlockSpec((groups, 1, share, u), lambda i, r: (0,...]
    ppermute x0 -> x13, starting transfers between devices: none -> 34.2 us  [shift(): return lax.ppermute(a, axis, [(i, (i + step) % n) for i in range(n)])]
    all_to_all x3 -> x2, blocking collectives: 206 us -> 173 us  [exchange(): return lax.all_to_all(a, axis, split_axis=0, concat_axis=0, tiled=True)]
    reshape x2 -> x8, local copies, waits for them, and re-layouts: 25.9 us -> 1.65 us  [the longest x4 1.35 us: widen(): jnp.repeat(jnp.repeat(t, 8, axis=0), 8, axis=1)]
    transpose x1 -> x0, other arithmetic: 5.98 us -> none  [z_weight(): wide = jnp.einsum('kz,ab->kazb', table, eye).reshape(k * 8, z * 8)]
    convert_element_type x2 -> x3, other arithmetic: 17.9 us -> 18.1 us  [cas_table(): return (jnp.cos(angle) + jnp.sin(angle)).astype(BF)]
  transfers between devices with their start and end apart: 2 -> 15, of which waited for: 2 -> 3; matrix products, arithmetic and copies ran while one was open for 6% -> 1% of each run, Pallas kernels for 3% -> 13%
where the time goes in v2:
time: 531 us; the launch traced here: 529 us
  waiting for transfers between devices  175 us (33%)
  blocking collectives  173 us (33%)
  Pallas kernels  109 us (21%)
  starting transfers between devices  44.4 us (8%)
  other arithmetic  20.8 us (4%)
  local copies, waits for them, and re-layouts  6.34 us (1%)
    all_to_all x2, blocking collectives, exchange(): return lax.all_to_all(a, axis, split_axis=0, concat_axis=0, tiled=True)  173 us
    ppermute x13, waiting for transfers between devices, shift(): return lax.ppermute(a, axis, [(i, (i + step) % n) for i in range(n)])  142 us
    pallas_call x8, Pallas kernels, x_inverse(): on_rank(body, (z,), [pl.BlockSpec((groups, 1, share, u), lambda i, r: (0,...  34.2 us
    ppermute x13, starting transfers between devices, shift(): return lax.ppermute(a, axis, [(i, (i + step) % n) for i in range(n)])  34.2 us
    all_to_all x2, waiting for transfers between devices, exchange(): return lax.all_to_all(a, axis, split_axis=0, concat_axis=0, tiled=True)  32.8 us
    pallas_call x8, Pallas kernels, green_piece(): on_rank(body, (k // cut,), [pl.BlockSpec((cut, 1, share, u), lambda i, r:...  28.8 us
    convert_element_type x3, other arithmetic, cas_table(): return (jnp.cos(angle) + jnp.sin(angle)).astype(BF)  18.1 us
    pallas_call x1, Pallas kernels, z_weight(): pl.pallas_call(body, grid=(v // rows, u // lanes), in_specs=[pl.BlockSpec...  13.2 us
  transfers between devices with their start and end apart: 15, of which 3 were waited for; matrix products, arithmetic and copies ran while one was open for 1% of the time, Pallas kernels for 13%

profile of v2, /device:TPU:0, one launch (start us, length us, event | category | flops | bytes accessed | tf_op | source)
XLA Modules:
  0.0 528.6 jit_solution(11848845759327257671)
XLA Ops:
  0.0 17.6 %add_convert_fusion.t_ref.refs_1_.refs_4_.refs_5_.refs_6_.refs_7_ = bf16[1024,1024]{1,0:T(8,128)(2,1)} fusion(), kind=kLoop, calls=%fused_computation.6 | loop fusion | flops 16777216 | bytes 2097152 | tf_op jit(solution)/shard_map/convert_element_type | solution.py:19
  17.6 10.2 %y_forward.1 = bf16[4,8,256,256]{3,2,1,0:T(8,128)(2,1)} custom-call(bf16[8,256,1024]{2,1,0:T(8,128)(2,1)} %d_ref.1, bf16[1024,1024]{1,0:T(8,128)(2,1)} %add_convert_fusion.t_ref.refs_1_.refs_4_.refs_5_.refs_6_.refs_7_), custom_call_target="tpu_custom_call" | custom-call | flops 4294967296 | bytes 10485760 | tf_op jit(solution)/shard_map/y_forward/pallas_call | solution.py:88
  27.8 54.5 %all_to_all.20.m_ref = bf16[4,8,256,256]{3,2,1,0:T(8,128)(2,1)} all-to-all(bf16[4,8,256,256]{3,2,1,0:T(8,128)(2,1)} %y_forward.1), channel_id=1, replica_groups=mesh['gz'=8,'pa'=4] {'pa'}, dimensions={0} | all-to-all | bytes 8388608 | tf_op jit(solution)/shard_map/all_to_all | solution.py:245
  82.3 10.0 %x_forward.1 = bf16[8,8,32,1024]{3,2,1,0:T(8,128)(2,1)} custom-call(bf16[4,8,256,256]{3,2,1,0:T(8,128)(2,1)} %all_to_all.20.m_ref, bf16[1024,1024]{1,0:T(8,128)(2,1)} %add_convert_fusion.t_ref.refs_1_.refs_4_.refs_5_.refs_6_.refs_7_), custom_call_target="tpu_custom_call" | custom-call | flops 4294967296 | bytes 10485760 | tf_op jit(solution)/shard_map/x_forward/pallas_call | solution.py:116
  92.3 6.7 %all-to-all-start.1 = ((bf16[8,8,32,1024]{3,2,1,0:T(8,128)(2,1)}), bf16[8,8,32,1024]{3,2,1,0:T(8,128)(2,1)}, u32[]{:S(2)}, u32[]{:S(2)}) async-start(bf16[8,8,32,1024]{3,2,1,0:T(8,128)(2,1)} %x_forward.1), calls=%async_computation.1 | async-start | bytes 8388608 | tf_op jit(solution)/shard_map/all_to_all | solution.py:245
  99.0 3.6 shard_map.37
  102.5 2.0 collective-permute-start
  104.5 3.6 shard_map.38
  108.2 1.5 collective-permute-start.1
  109.6 3.6 shard_map.39
  113.2 2.4 collective-permute-start.2
  115.6 3.6 shard_map.40
  119.2 1.5 collective-permute-start.3
  120.7 3.6 shard_map.41
  124.2 2.4 collective-permute-start.4
  126.6 3.6 shard_map.42
  130.2 3.6 shard_map.43
  134.0 0.3 add_convert_fusion.1
  134.8 60.7 %collective-permute-done.refs_0_ = bf16[16,32,1024]{2,1,0:T(8,128)(2,1)S(1)} collective-permute-done((bf16[16,32,1024]{2,1,0:T(8,128)(2,1)}, bf16[16,32,1024]{2,1,0:T(8,128)(2,1)S(1)}, u32[]{:S(2)}, u32[]{:S(2)}) %collective-permute-start) | collective-permute-done | bytes 1048608 | tf_op jit(solution)/shard_map/ppermute | solution.py:75
  195.8 0.8 copy-done.6
  196.5 21.0 %collective-permute-start.6 = (bf16[16,32,1024]{2,1,0:T(8,128)(2,1)}, bf16[16,32,1024]{2,1,0:T(8,128)(2,1)}, u32[]{:S(2)}, u32[]{:S(2)}) collective-permute-start(bf16[16,32,1024]{2,1,0:T(8,128)(2,1)} %shard_map.43), channel_id=1, source_target_pairs={{0,28},{4,0},{8,4},{12,8},{16,12},{20,16},{24,20},{28,24},{1,29},{... | collective-permute-start | bytes 3145736 | tf_op jit(solution)/shard_map/ppermute | solution.py:75
  217.6 3.6 shard_map.44.refs_7_
  221.2 0.5 copy.8
  222.0 0.5 copy.10
  222.6 1.3 compare_select_fusion.1.refs_8_
  223.9 1.3 compare_select_fusion.refs_9_
  225.2 81.0 %collective-permute-done.2.refs_2_ = bf16[16,32,1024]{2,1,0:T(8,128)(2,1)} collective-permute-done((bf16[16,32,1024]{2,1,0:T(8,128)(2,1)}, bf16[16,32,1024]{2,1,0:T(8,128)(2,1)}, u32[]{:S(2)}, u32[]{:S(2)}) %collective-permute-start.2) | collective-permute-done | bytes 1048608 | tf_op jit(solution)/shard_map/ppermute | solution.py:75
  306.2 13.2 %z_weight.1 = (bf16[8,4,32,1024]{3,2,1,0:T(8,128)(2,1)}, bf16[8,4,32,1024]{3,2,1,0:T(8,128)(2,1)}) custom-call(bf16[64,32,1024]{2,1,0:T(8,128)(2,1)} %bitcast.1.s_ref, bf16[16,32,1024]{2,1,0:T(8,128)(2,1)} %copy-done.6, bf16[16,32,1024]{2,1,0:T(8,128)(2,1)} %copy-done.7, bf16[16,32,1024]{2,1,0:T(8,128)(2,1)} %collective-permute-done.2.refs_2_, ...), custom_call_target="tpu_custom_call" | custom-call | flops 8589934592 | bytes 16777216 | tf_op jit(solution)/shard_map/z_weight/pallas_call | solution.py:170
  319.4 118.5 %all_to_all.21.refs_0_ = bf16[8,4,32,1024]{3,2,1,0:T(8,128)(2,1)} all-to-all(bf16[8,4,32,1024]{3,2,1,0:T(8,128)(2,1)} %get-tuple-element.8), channel_id=1, replica_groups=mesh['gz'=8,'pa'=4] {'gz'}, dimensions={0} | all-to-all | bytes 4194304 | tf_op jit(solution)/shard_map/all_to_all | solution.py:245
  437.9 3.6 all-to-all-start.2
  441.5 4.3 shard_map.50
  445.8 4.3 shard_map.51
  450.1 0.8 collective-permute-start.11
  450.9 4.3 shard_map.52
  455.1 1.4 collective-permute-start.12
  456.6 32.8 %all-to-all-done.2.refs_0_ = bf16[8,4,32,1024]{3,2,1,0:T(8,128)(2,1)S(1)} async-done(((bf16[8,4,32,1024]{3,2,1,0:T(8,128)(2,1)}), bf16[8,4,32,1024]{3,2,1,0:T(8,128)(2,1)S(1)}, u32[]{:S(2)}, u32[]{:S(2)}) %all-to-all-start.2) | async-done | bytes 2097184 | tf_op jit(solution)/shard_map/all_to_all | solution.py:245
  489.4 1.3 copy-done
  490.7 4.3 shard_map.48
  495.0 4.3 shard_map.47
  499.3 0.8 collective-permute-start.8
  500.1 4.2 shard_map.46
  504.5 4.3 shard_map.49.refs_0_
  508.8 4.3 shard_map.45.refs_0_
  513.1 0.8 copy-done.3
  513.9 6.5 %shard_map.53.refs_8_ = f32[8,256,1024]{2,1,0:T(8,128)} custom-call(s32[1]{0:T(128)} %bitcast.r, bf16[4,256,256]{2,1,0:T(8,128)(2,1)} %shard_map.49.refs_0_, bf16[4,256,256]{2,1,0:T(8,128)(2,1)} %copy-done.1, bf16[4,256,256]{2,1,0:T(8,128)(2,1)} %copy-done.3, bf16[4,256,256]{2,1,0:T(8,128)(2,1)} %collective-permute-done.12.refs_3_, ...), custom_call_target="tpu_custom_call" | custom-call | flops 2147483648 | bytes 6291456 | tf_op jit(solution)/shard_map/pallas_call | solution.py:233
  520.4 0.7 copy-done.2
  521.3 0.8 copy-done.5
  522.1 6.5 %shard_map.54 = f32[8,256,1024]{2,1,0:T(8,128)} custom-call(s32[1]{0:T(128)} %bitcast.r, bf16[4,256,256]{2,1,0:T(8,128)(2,1)} %shard_map.45.refs_0_, bf16[4,256,256]{2,1,0:T(8,128)(2,1)} %copy-done.5, bf16[4,256,256]{2,1,0:T(8,128)(2,1)} %copy-done.4, bf16[4,256,256]{2,1,0:T(8,128)(2,1)} %copy-done.2, ...), custom_call_target="tpu_custom_call", output_to_operand_aliasing={{}: (9, {})} | custom-call | flops 2147483648 | bytes 6291456 | tf_op jit(solution)/shard_map/pallas_call | solution.py:233
  (41 shorter events, 1.6 us)
Async XLA Ops:
  92.3 213.8 %all-to-all-start.1 = ((bf16[8,8,32,1024]{3,2,1,0:T(8,128)(2,1)}), bf16[8,8,32,1024]{3,2,1,0:T(8,128)(2,1)}, u32[]{:S(2)}, u32[]{:S(2)}) async-start(bf16[8,8,32,1024]{3,2,1,0:T(8,128)(2,1)} %x_forward.1), calls=%async_computation.1 | async-start | bytes 8388608 | tf_op jit(solution)/shard_map/all_to_all | solution.py:245
  102.5 93.0 %collective-permute-start = (bf16[16,32,1024]{2,1,0:T(8,128)(2,1)}, bf16[16,32,1024]{2,1,0:T(8,128)(2,1)S(1)}, u32[]{:S(2)}, u32[]{:S(2)}) collective-permute-start(bf16[16,32,1024]{2,1,0:T(8,128)(2,1)} %shard_map.37), channel_id=1, source_target_pairs={{0,4},{4,8},{8,12},{12,16},{16,20},{20,24},{24,28},{28,0},{1,5},{5... | collective-permute-start | bytes 3145736 | tf_op jit(solution)/shard_map/ppermute | solution.py:75
  108.2 87.6 %collective-permute-start.1 = (bf16[16,32,1024]{2,1,0:T(8,128)(2,1)}, bf16[16,32,1024]{2,1,0:T(8,128)(2,1)S(1)}, u32[]{:S(2)}, u32[]{:S(2)}) collective-permute-start(bf16[16,32,1024]{2,1,0:T(8,128)(2,1)} %shard_map.38), channel_id=1, source_target_pairs={{0,8},{4,12},{8,16},{12,20},{16,24},{20,28},{24,0},{28,4},{1,9},{5... | collective-permute-start | bytes 3145736 | tf_op jit(solution)/shard_map/ppermute | solution.py:75
  113.2 192.9 %collective-permute-start.2 = (bf16[16,32,1024]{2,1,0:T(8,128)(2,1)}, bf16[16,32,1024]{2,1,0:T(8,128)(2,1)}, u32[]{:S(2)}, u32[]{:S(2)}) collective-permute-start(bf16[16,32,1024]{2,1,0:T(8,128)(2,1)} %shard_map.39), channel_id=1, source_target_pairs={{0,12},{4,16},{8,20},{12,24},{16,28},{20,0},{24,4},{28,8},{1,13},{... | collective-permute-start | bytes 3145736 | tf_op jit(solution)/shard_map/ppermute | solution.py:75
  119.2 186.9 %collective-permute-start.3 = (bf16[16,32,1024]{2,1,0:T(8,128)(2,1)}, bf16[16,32,1024]{2,1,0:T(8,128)(2,1)}, u32[]{:S(2)}, u32[]{:S(2)}) collective-permute-start(bf16[16,32,1024]{2,1,0:T(8,128)(2,1)} %shard_map.40), channel_id=1, source_target_pairs={{0,16},{4,20},{8,24},{12,28},{16,0},{20,4},{24,8},{28,12},{1,17},{... | collective-permute-start | bytes 3145736 | tf_op jit(solution)/shard_map/ppermute | solution.py:75
  124.2 181.9 %collective-permute-start.4 = (bf16[16,32,1024]{2,1,0:T(8,128)(2,1)}, bf16[16,32,1024]{2,1,0:T(8,128)(2,1)}, u32[]{:S(2)}, u32[]{:S(2)}) collective-permute-start(bf16[16,32,1024]{2,1,0:T(8,128)(2,1)} %shard_map.41), channel_id=1, source_target_pairs={{0,20},{4,24},{8,28},{12,0},{16,4},{20,8},{24,12},{28,16},{1,21},{... | collective-permute-start | bytes 3145736 | tf_op jit(solution)/shard_map/ppermute | solution.py:75
  130.2 3.6 copy-start.8
  195.5 1.0 copy-start.6
  195.6 110.6 %collective-permute-start.5 = (bf16[16,32,1024]{2,1,0:T(8,128)(2,1)}, bf16[16,32,1024]{2,1,0:T(8,128)(2,1)}, u32[]{:S(2)}, u32[]{:S(2)}) collective-permute-start(bf16[16,32,1024]{2,1,0:T(8,128)(2,1)} %shard_map.42), channel_id=1, source_target_pairs={{0,24},{4,28},{8,0},{12,4},{16,8},{20,12},{24,16},{28,20},{1,25},{... | collective-permute-start | bytes 3145736 | tf_op jit(solution)/shard_map/ppermute | solution.py:75
  196.5 24.7 %copy-start.7 = (bf16[16,32,1024]{2,1,0:T(8,128)(2,1)}, bf16[16,32,1024]{2,1,0:T(8,128)(2,1)S(1)}, u32[]{:S(2)}) copy-start(bf16[16,32,1024]{2,1,0:T(8,128)(2,1)S(1)} %collective-permute-done.1.refs_1_) | copy-start | bytes 3145732
  196.5 109.6 %collective-permute-start.6 = (bf16[16,32,1024]{2,1,0:T(8,128)(2,1)}, bf16[16,32,1024]{2,1,0:T(8,128)(2,1)}, u32[]{:S(2)}, u32[]{:S(2)}) collective-permute-start(bf16[16,32,1024]{2,1,0:T(8,128)(2,1)} %shard_map.43), channel_id=1, source_target_pairs={{0,28},{4,0},{8,4},{12,8},{16,12},{20,16},{24,20},{28,24},{1,29},{... | collective-permute-start | bytes 3145736 | tf_op jit(solution)/shard_map/ppermute | solution.py:75
  437.9 51.5 %all-to-all-start.2 = ((bf16[8,4,32,1024]{3,2,1,0:T(8,128)(2,1)}), bf16[8,4,32,1024]{3,2,1,0:T(8,128)(2,1)S(1)}, u32[]{:S(2)}, u32[]{:S(2)}) async-start(bf16[8,4,32,1024]{3,2,1,0:T(8,128)(2,1)} %get-tuple-element.7), calls=%async_computation.2 | async-start | bytes 4194304 | tf_op jit(solution)/shard_map/all_to_all | solution.py:245
  445.8 58.5 %collective-permute-start.10 = (bf16[4,256,256]{2,1,0:T(8,128)(2,1)}, bf16[4,256,256]{2,1,0:T(8,128)(2,1)S(1)}, u32[]{:S(2)}, u32[]{:S(2)}) collective-permute-start(bf16[4,256,256]{2,1,0:T(8,128)(2,1)} %shard_map.50), channel_id=1, source_target_pairs={{0,1},{1,2},{2,3},{3,0},{4,5},{5,6},{6,7},{7,4},{8,9},{9,10},{10,1... | collective-permute-start | bytes 1572872 | tf_op jit(solution)/shard_map/ppermute | solution.py:75
  450.1 63.0 %collective-permute-start.11 = (bf16[4,256,256]{2,1,0:T(8,128)(2,1)}, bf16[4,256,256]{2,1,0:T(8,128)(2,1)S(1)}, u32[]{:S(2)}, u32[]{:S(2)}) collective-permute-start(bf16[4,256,256]{2,1,0:T(8,128)(2,1)} %shard_map.51), channel_id=1, source_target_pairs={{0,2},{1,3},{2,0},{3,1},{4,6},{5,7},{6,4},{7,5},{8,10},{9,11},{10,... | collective-permute-start | bytes 1572872 | tf_op jit(solution)/shard_map/ppermute | solution.py:75
  455.1 57.9 %collective-permute-start.12 = (bf16[4,256,256]{2,1,0:T(8,128)(2,1)}, bf16[4,256,256]{2,1,0:T(8,128)(2,1)}, u32[]{:S(2)}, u32[]{:S(2)}) collective-permute-start(bf16[4,256,256]{2,1,0:T(8,128)(2,1)} %shard_map.52), channel_id=1, source_target_pairs={{0,3},{1,0},{2,1},{3,2},{4,7},{5,4},{6,5},{7,6},{8,11},{9,8},{10,9... | collective-permute-start | bytes 1572872 | tf_op jit(solution)/shard_map/ppermute | solution.py:75
  489.4 1.3 copy-start
  495.0 25.4 %collective-permute-start.9 = (bf16[4,256,256]{2,1,0:T(8,128)(2,1)}, bf16[4,256,256]{2,1,0:T(8,128)(2,1)S(1)}, u32[]{:S(2)}, u32[]{:S(2)}) collective-permute-start(bf16[4,256,256]{2,1,0:T(8,128)(2,1)} %shard_map.48), channel_id=1, source_target_pairs={{0,3},{1,0},{2,1},{3,2},{4,7},{5,4},{6,5},{7,6},{8,11},{9,8},{10,9... | collective-permute-start | bytes 1572872 | tf_op jit(solution)/shard_map/ppermute | solution.py:75
  499.3 21.1 %collective-permute-start.8 = (bf16[4,256,256]{2,1,0:T(8,128)(2,1)}, bf16[4,256,256]{2,1,0:T(8,128)(2,1)S(1)}, u32[]{:S(2)}, u32[]{:S(2)}) collective-permute-start(bf16[4,256,256]{2,1,0:T(8,128)(2,1)} %shard_map.47), channel_id=1, source_target_pairs={{0,2},{1,3},{2,0},{3,1},{4,6},{5,7},{6,4},{7,5},{8,10},{9,11},{10,... | collective-permute-start | bytes 1572872 | tf_op jit(solution)/shard_map/ppermute | solution.py:75
  504.3 8.7 %copy-start.1 = (bf16[4,256,256]{2,1,0:T(8,128)(2,1)}, bf16[4,256,256]{2,1,0:T(8,128)(2,1)S(1)}, u32[]{:S(2)}) copy-start(bf16[4,256,256]{2,1,0:T(8,128)(2,1)S(1)} %collective-permute-done.10.refs_1_) | copy-start | bytes 1572868
  504.3 16.1 %collective-permute-start.7 = (bf16[4,256,256]{2,1,0:T(8,128)(2,1)}, bf16[4,256,256]{2,1,0:T(8,128)(2,1)S(1)}, u32[]{:S(2)}, u32[]{:S(2)}) collective-permute-start(bf16[4,256,256]{2,1,0:T(8,128)(2,1)} %shard_map.46), channel_id=1, source_target_pairs={{0,1},{1,2},{2,3},{3,0},{4,5},{5,6},{6,7},{7,4},{8,9},{9,10},{10,1... | collective-permute-start | bytes 1572872 | tf_op jit(solution)/shard_map/ppermute | solution.py:75
  513.1 0.8 copy-start.3
  520.4 0.8 copy-start.2
  520.4 1.0 copy-start.4
  521.3 0.8 copy-start.5
